TPU v7x, 32 devices: a whole 2x2x4 slice. The times are simulated.
32 devices in a mesh: gx: 8 (over z, x), gy: 4 (over y, core).
Axes of the slice: x: 2, y: 2, z: 4, core: 2. Of those that a mesh axis runs over, the one named last changes fastest.
Arguments:
- velocity: float32 [2, 1024, 1024], P(None, 'gy', 'gx'), may hold values from -3 to 3
- stress: float32 [3, 1024, 1024], P(None, 'gy', 'gx'), may hold values from -3 to 3
- ice_mass: float32 [1024, 1024], P('gy', 'gx'), may hold values from 0.5 to 4
- strength: float32 [1024, 1024], P('gy', 'gx'), may hold values from 0.2 to 2
- land_mask: int32 [1024, 1024], P('gy', 'gx'), may hold values from 0 to 1
- ocean_forcing: float32 [4, 1024, 1024], P(None, ('gy', 'gx')), may hold values from -3 to 3
Outputs:
- velocity_out: float32 [2, 1024, 1024], P(None, 'gy', 'gx')
- stress_out: float32 [3, 1024, 1024], P(None, 'gy', 'gx')
- residuals: float32 [4], replicated
- ocean_stress: float32 [2, 1024, 1024], P(None, ('gy', 'gx'))
All inputs are finite; a program needn't handle non-finite values.
Results may differ from a plain program's by a relative error of at most 0.0001.
Values sent between devices are 32-bit elements; how exact they have to be, the bound alone decides.
A program may use at most 64 MiB of HBM per device.

v0:
```python
import jax
import jax.numpy as jnp
from jax import lax
from jax.sharding import PartitionSpec as P

ITERS = 4


ALPHA = 4.0
BETA = 4.0
WATER_DRAG = 1.0
DELTA_FLOOR = 0.0025


def extended(cells, sides, width):
    for axis, dim in sides:
        count = lax.axis_size(axis)
        head = lax.slice_in_dim(cells, 0, width, axis=dim)
        tail = lax.slice_in_dim(cells, cells.shape[dim] - width, cells.shape[dim], axis=dim)
        cells = jnp.concatenate(
            [
                lax.ppermute(tail, axis, [(i, (i + 1) % count) for i in range(count)]),
                cells,
                lax.ppermute(head, axis, [((i + 1) % count, i) for i in range(count)]),
            ],
            axis=dim,
        )
    return cells


def diff_east(padded):
    return 0.5 * (padded[..., 1:-1, 2:] - padded[..., 1:-1, :-2])


def diff_north(padded):
    return 0.5 * (padded[..., 2:, 1:-1] - padded[..., :-2, 1:-1])


def trim_edges(field, level):
    if level == 0:
        return field
    return field[..., level:-level, level:-level]


def record_sum(own_sum, global_sums):
    global_sums.append(lax.psum(own_sum, ("gx", "gy")))


def relax_stress(padded_vel, stress, strength, ice_frac):
    east_dx = diff_east(padded_vel[0])
    east_dy = diff_north(padded_vel[0])
    north_dx = diff_east(padded_vel[1])
    north_dy = diff_north(padded_vel[1])
    divergence = east_dx + north_dy
    tension = east_dx - north_dy
    shear_rate = east_dy + north_dx
    delta_rate = jnp.sqrt(
        divergence * divergence + 0.25 * (tension * tension + shear_rate * shear_rate) + DELTA_FLOOR
    )
    target = jnp.stack(
        [
            strength * (divergence / delta_rate - 1.0),
            strength * tension / (4.0 * delta_rate),
            strength * shear_rate / (8.0 * delta_rate),
        ]
    )
    return (stress + (target - stress) / ALPHA) * ice_frac


def drag_coeff(vel, currents):
    east_gap = currents[0] - vel[0]
    north_gap = currents[1] - vel[1]
    return WATER_DRAG * jnp.sqrt(east_gap * east_gap + north_gap * north_gap + 0.01)


def relax_velocity(padded_stress, vel, vel_start, forcing, ice_mass, coriolis, ice_frac):
    normal_xx = 0.5 * (padded_stress[0] + padded_stress[1])
    normal_yy = 0.5 * (padded_stress[0] - padded_stress[1])
    shear_xy = padded_stress[2]
    force_east = diff_east(normal_xx) + diff_north(shear_xy)
    force_north = diff_east(shear_xy) + diff_north(normal_yy)
    drag_rate = drag_coeff(vel, forcing[2:4])
    denominator = BETA + 1.0 + drag_rate / ice_mass
    new_east = (
        (
            BETA * vel[0]
            + vel_start[0]
            + (force_east + forcing[0] + drag_rate * forcing[2]) / ice_mass
            + coriolis * vel[1]
        )
        / denominator
        * ice_frac
    )
    new_north = (
        (
            BETA * vel[1]
            + vel_start[1]
            + (force_north + forcing[1] + drag_rate * forcing[3]) / ice_mass
            - coriolis * vel[0]
        )
        / denominator
        * ice_frac
    )
    return jnp.stack([new_east, new_north])


def local(velocity, stress, ice_mass, strength, land_mask, ocean_forcing):
    row_count = velocity.shape[1]
    col_count = velocity.shape[2]
    forcing = lax.all_to_all(ocean_forcing, "gx", split_axis=2, concat_axis=1, tiled=True)
    ice_frac = land_mask.astype(jnp.float32)
    lat_band = lax.axis_index("gy")
    total_rows = lax.axis_size("gy") * row_count
    global_sums = []
    depth = 2 * ITERS
    stacked = jnp.concatenate(
        [velocity, stress, strength[None], ice_mass[None], ice_frac[None], forcing], axis=0
    )
    padded = extended(stacked, (("gx", 2), ("gy", 1)), depth)
    wide_rows = lat_band * row_count - depth + jnp.arange(row_count + 2 * depth, dtype=jnp.int32)
    inside = ((wide_rows >= 0) & (wide_rows < total_rows)).astype(jnp.float32)[:, None]
    wide_vel = padded[0:2] * inside
    wide_stress = padded[2:5] * inside
    wide_strength = padded[5]
    wide_mass = padded[6]
    wide_ice = padded[7] * inside
    wide_forcing = padded[8:12]
    wide_lat = wide_rows.astype(jnp.float32)
    wide_coriolis = jnp.broadcast_to(
        (0.3 + 1.2 * (wide_lat + 0.5) / total_rows)[:, None],
        (row_count + 2 * depth, col_count + 2 * depth),
    )
    vel_work = wide_vel
    stress_work = wide_stress
    margin = depth
    for subcycle in range(ITERS):
        level_one = depth - (margin - 1)
        stress_cut = (stress_work.shape[-1] - (col_count + 2 * (margin - 1))) // 2
        stress_work = relax_stress(
            vel_work,
            trim_edges(stress_work, stress_cut),
            trim_edges(wide_strength, level_one),
            trim_edges(wide_ice, level_one),
        )
        level_two = depth - (margin - 2)
        old_vel = trim_edges(vel_work, 2)
        new_vel = relax_velocity(
            stress_work,
            old_vel,
            trim_edges(wide_vel, level_two),
            trim_edges(wide_forcing, level_two),
            trim_edges(wide_mass, level_two),
            trim_edges(wide_coriolis, level_two),
            trim_edges(wide_ice, level_two),
        )
        change = trim_edges(new_vel - old_vel, margin - 2)
        record_sum(jnp.sum(change * change), global_sums)
        vel_work = new_vel
        margin = margin - 2
    stress = trim_edges(stress_work, 1)
    history = jnp.stack(global_sums)
    drag_rate = drag_coeff(vel_work, forcing[2:4])
    ice_stress = drag_rate * (vel_work - forcing[2:4]) * ice_frac
    ocean_stress = lax.all_to_all(ice_stress, "gx", split_axis=1, concat_axis=2, tiled=True)
    return (vel_work, stress, history, ocean_stress)


def solution(mesh):
    placed = (
        P(None, "gy", "gx"),
        P(None, "gy", "gx"),
        P("gy", "gx"),
        P("gy", "gx"),
        P("gy", "gx"),
        P(None, ("gy", "gx"), None),
    )
    return jax.shard_map(
        local,
        mesh=mesh,
        in_specs=placed,
        out_specs=(P(None, "gy", "gx"), P(None, "gy", "gx"), P(), P(None, ("gy", "gx"), None)),
        check_vma=False,
    )
```

profile of v0, /device:TPU:0, one launch (start us, length us, event | category | flops | bytes accessed | tf_op | source)
XLA Modules:
  0.0 124.1 jit_solution(12943327118963534328)
XLA Ops:
  0.6 1.8 %copy.37 = f32[4,32,1024]{1,0,2:T(4,128)S(1)} copy(f32[4,32,1024]{2,1,0:T(8,128)} %param.11) | data formatting | bytes 1048576 | tf_op args[5]
  2.4 2.2 %reshape.95 = f32[8,1,16384]{2,1,0:T(1,128)} reshape(f32[1024,4,32]{2,1,0:T(4,128)S(1)} %bitcast.395) | data formatting | bytes 1048576
  4.6 7.4 %all-to-all-start = ((f32[8,1,16384]{2,1,0:T(1,128)}), f32[8,1,16384]{2,1,0:T(1,128)S(1)}, u32[]{:S(2)}, u32[]{:S(2)}) async-start(f32[8,1,16384]{2,1,0:T(1,128)} %reshape.95), calls=%async_computation | async-start | bytes 1048576 | tf_op jit(solution)/shard_map/all_to_all | solution.py:110
  12.2 1.0 constant_dynamic-update-slice_fusion.2
  13.5 13.0 %all-to-all-done = f32[8,1,16384]{2,1,0:T(1,128)S(1)} async-done(((f32[8,1,16384]{2,1,0:T(1,128)}), f32[8,1,16384]{2,1,0:T(1,128)S(1)}, u32[]{:S(2)}, u32[]{:S(2)}) %all-to-all-start) | async-done | bytes 524320 | tf_op jit(solution)/shard_map/all_to_all | solution.py:110
  27.0 1.9 %reduce.6 = f32[8,16384]{1,0:T(8,128)S(1)} reduce(f32[8,1,16384]{2,1,0:T(1,128)S(1)} %all-to-all-done, f32[]{:T(128)} %broadcast.256), dimensions={1}, to_apply=%all_to_all.26.reduce_sub_computation | reduce | bytes 1048580 | tf_op jit(solution)/shard_map/all_to_all | solution.py:110
  28.9 2.4 %reshape.96 = f32[1024,4,32]{2,1,0:T(4,128)} reshape(f32[8,16384]{1,0:T(8,128)S(1)} %reduce.6) | data formatting | bytes 1048576
  31.3 1.8 %copy.52 = f32[4,32,8,128]{3,1,2,0:T(8,128)S(1)} copy(f32[4,32,8,128]{1,0,3,2:T(4,128)} %bitcast.377) | data formatting | bytes 1048576 | tf_op jit(solution)/shard_map/all_to_all | solution.py:110
  33.2 1.7 %fusion.160 = (f32[12,256,8]{2,1,0:T(8,128)S(1)}, f32[12,256,8]{2,1,0:T(8,128)}) fusion(f32[12,256,128]{2,1,0:T(8,128)S(1)} %constant_dynamic-update-slice_fusion), kind=kLoop, calls=%fused_computation.288 | loop fusion | bytes 393216 | tf_op jit(solution)/shard_map/slice | solution.py:19
  34.9 1.8 %copy.41 = f32[12,256,8]{1,2,0:T(8,128)S(1)} copy(f32[12,256,8]{2,1,0:T(8,128)} %get-tuple-element.42) | data formatting | bytes 196608 | tf_op jit(solution)/shard_map/slice | solution.py:18
  36.7 2.4 %collective-permute-start.1 = (f32[12,256,8]{1,2,0:T(8,128)S(1)}, f32[12,256,8]{1,2,0:T(8,128)S(1)}, u32[]{:S(2)}, u32[]{:S(2)}) collective-permute-start(f32[12,256,8]{1,2,0:T(8,128)S(1)} %copy.41), channel_id=1, source_target_pairs={{4,0},{8,4},{12,8},{16,12},{20,16},{24,20},{28,24},{0,28},{5,1},{9... | collective-permute-start | bytes 294920 | tf_op jit(solution)/shard_map/ppermute | solution.py:24
  39.1 1.1 copy.40
  40.3 3.0 %copy.51 = f32[4,32,8,128]{3,2,1,0:T(8,128)} copy(f32[4,32,8,128]{1,0,3,2:T(4,128)} %bitcast.378) | data formatting | bytes 1048576 | tf_op jit(solution)/shard_map/all_to_all | solution.py:110
  43.8 4.1 %collective-permute-done = f32[12,256,8]{1,2,0:T(8,128)} collective-permute-done((f32[12,256,8]{1,2,0:T(8,128)}, f32[12,256,8]{1,2,0:T(8,128)}, u32[]{:S(2)}, u32[]{:S(2)}) %collective-permute-start) | collective-permute-done | bytes 98336 | tf_op jit(solution)/shard_map/ppermute | solution.py:22
  47.8 2.5 %copy.42 = f32[12,256,8]{2,1,0:T(8,128)} copy(f32[12,256,8]{1,2,0:T(8,128)} %collective-permute-done) | data formatting | bytes 196608 | tf_op jit(solution)/shard_map/ppermute | solution.py:22
  50.4 1.0 pad_maximum_fusion.7
  52.2 1.4 %collective-permute-done.3 = f32[12,8,144]{2,1,0:T(8,128)S(1)} collective-permute-done((f32[12,8,144]{2,1,0:T(8,128)S(1)}, f32[12,8,144]{2,1,0:T(8,128)S(1)}, u32[]{:S(2)}, u32[]{:S(2)}) %collective-permute-start.3) | collective-permute-done | bytes 55328 | tf_op jit(solution)/shard_map/ppermute | solution.py:24
  53.7 2.9 %collective-permute-done.2 = f32[12,8,144]{2,1,0:T(8,128)S(1)} collective-permute-done((f32[12,8,144]{2,1,0:T(8,128)S(1)}, f32[12,8,144]{2,1,0:T(8,128)S(1)}, u32[]{:S(2)}, u32[]{:S(2)}) %collective-permute-start.2) | collective-permute-done | bytes 55328 | tf_op jit(solution)/shard_map/ppermute | solution.py:22
  56.6 1.3 %pad_maximum_fusion = f32[12,272,144]{2,1,0:T(8,128)S(1)} fusion(f32[12,8,144]{2,1,0:T(8,128)S(1)} %collective-permute-done.3, f32[12,256,8]{2,1,0:T(8,128)S(1)} %copy.43, f32[12,256,128]{2,1,0:T(8,128)S(1)} %constant_dynamic-update-slice_fusion, f32[12,256,8]{2,1,0:T(8,128)S(1)} %copy-done.2, f32[12,8,144]{2,1,0:T(8,128)S(1)} %collective-permute-done.2), kind=kLoop, calls=%fused_computation | loop fusion | flops 1880064 | bytes 3760128 | tf_op jit(solution)/shard_map/concatenate | solution.py:20
  58.7 0.9 copy-done
  61.9 1.5 %copy-done.1 = f32[12,272,144]{2,1,0:T(8,128)S(1)} copy-done((f32[12,272,144]{2,1,0:T(8,128)S(1)}, f32[12,272,144]{2,1,0:T(8,128)}, u32[]{:S(2)}) %copy-start.1) | copy-done | bytes 1880088
  63.4 0.9 fusion.19
  66.4 0.9 fusion.71
  67.3 0.9 fusion.83
  69.5 0.9 fusion.48
  70.4 0.9 fusion.59
  73.4 0.9 copy.49
  74.3 3.4 %all-to-all-start.1 = ((f32[2,256,128]{2,0,1:T(2,128)}), f32[2,256,128]{2,0,1:T(2,128)S(1)}, u32[]{:S(2)}, u32[]{:S(2)}) async-start(f32[2,256,128]{2,0,1:T(2,128)} %copy.49), calls=%async_computation.1 | async-start | bytes 524288 | tf_op jit(solution)/shard_map/all_to_all | solution.py:164
  78.0 1.2 fusion.98
  79.2 40.1 %all-reduce = (f32[1]{0:T(128)}, f32[1]{0:T(128)}, f32[1]{0:T(128)}, f32[1]{0:T(128)}) all-reduce(f32[1]{0:T(128)} %bitcast.78, f32[1]{0:T(128)} %bitcast.77, f32[1]{0:T(128)} %bitcast.76, f32[1]{0:T(128)} %bitcast.75), channel_id=1, replica_groups=mesh['gx'=8,'gy'=4] {'gx','gy'}, use_global_device_ids=true, to_apply=%region_7.0 | all-reduce | flops 4 | bytes 32 | tf_op jit(solution)/shard_map/psum | solution.py:46
  119.3 0.9 slice.886
  120.2 3.0 %pad_maximum_fusion.8 = f32[4]{0:T(128)} fusion(f32[1]{0:T(128)} %get-tuple-element.12, f32[1]{0:T(128)} %get-tuple-element.13, f32[1]{0:T(128)} %get-tuple-element.14, f32[1]{0:T(128)} %get-tuple-element.15), kind=kLoop, calls=%fused_computation.287 | loop fusion | flops 12 | bytes 32 | tf_op jit(solution)/shard_map/stack | solution.py:161
  (74 shorter events, 11.8 us)
Async XLA Ops:
  2.4 9.8 %copy-start.5 = (s32[256,128]{1,0:T(8,128)S(1)}, s32[256,128]{1,0:T(8,128)}, u32[]{:S(2)}) copy-start(s32[256,128]{1,0:T(8,128)} %param.10) | copy-start | bytes 393220
  4.6 8.8 %copy-start.6 = (f32[3,256,128]{2,1,0:T(8,128)S(1)}, f32[3,256,128]{2,1,0:T(8,128)}, u32[]{:S(2)}) copy-start(f32[3,256,128]{2,1,0:T(8,128)} %param.7) | copy-start | bytes 1179652
  4.6 8.8 %copy-start.7 = (f32[256,128]{1,0:T(8,128)S(1)}, f32[256,128]{1,0:T(8,128)}, u32[]{:S(2)}) copy-start(f32[256,128]{1,0:T(8,128)} %param.9) | copy-start | bytes 393220
  4.6 8.8 %copy-start.8 = (f32[256,128]{1,0:T(8,128)S(1)}, f32[256,128]{1,0:T(8,128)}, u32[]{:S(2)}) copy-start(f32[256,128]{1,0:T(8,128)} %param.8) | copy-start | bytes 393220
  4.6 21.9 %all-to-all-start = ((f32[8,1,16384]{2,1,0:T(1,128)}), f32[8,1,16384]{2,1,0:T(1,128)S(1)}, u32[]{:S(2)}, u32[]{:S(2)}) async-start(f32[8,1,16384]{2,1,0:T(1,128)} %reshape.95), calls=%async_computation | async-start | bytes 1048576 | tf_op jit(solution)/shard_map/all_to_all | solution.py:110
  36.7 6.5 %collective-permute-start.1 = (f32[12,256,8]{1,2,0:T(8,128)S(1)}, f32[12,256,8]{1,2,0:T(8,128)S(1)}, u32[]{:S(2)}, u32[]{:S(2)}) collective-permute-start(f32[12,256,8]{1,2,0:T(8,128)S(1)} %copy.41), channel_id=1, source_target_pairs={{4,0},{8,4},{12,8},{16,12},{20,16},{24,20},{28,24},{0,28},{5,1},{9... | collective-permute-start | bytes 294920 | tf_op jit(solution)/shard_map/ppermute | solution.py:24
  40.2 7.6 %collective-permute-start = (f32[12,256,8]{1,2,0:T(8,128)}, f32[12,256,8]{1,2,0:T(8,128)}, u32[]{:S(2)}, u32[]{:S(2)}) collective-permute-start(f32[12,256,8]{1,2,0:T(8,128)} %copy.40), channel_id=1, source_target_pairs={{0,4},{4,8},{8,12},{12,16},{16,20},{20,24},{24,28},{28,0},{1,5},{5... | collective-permute-start | bytes 294920 | tf_op jit(solution)/shard_map/ppermute | solution.py:22
  50.4 1.6 %copy-start.3 = (f32[4,32,8,128]{3,2,1,0:T(8,128)S(1)}, f32[4,32,8,128]{3,2,1,0:T(8,128)}, u32[]{:S(2)}) copy-start(f32[4,32,8,128]{3,2,1,0:T(8,128)} %copy.51) | copy-start | bytes 1572868
  51.4 2.3 %collective-permute-start.3 = (f32[12,8,144]{2,1,0:T(8,128)S(1)}, f32[12,8,144]{2,1,0:T(8,128)S(1)}, u32[]{:S(2)}, u32[]{:S(2)}) collective-permute-start(f32[12,8,144]{2,1,0:T(8,128)S(1)} %get-tuple-element.38), channel_id=1, source_target_pairs={{1,0},{2,1},{3,2},{0,3},{5,4},{6,5},{7,6},{4,7},{9,8},{10,9},{11,1... | collective-permute-start | bytes 165896 | tf_op jit(solution)/shard_map/ppermute | solution.py:24
  51.5 5.2 %collective-permute-start.2 = (f32[12,8,144]{2,1,0:T(8,128)S(1)}, f32[12,8,144]{2,1,0:T(8,128)S(1)}, u32[]{:S(2)}, u32[]{:S(2)}) collective-permute-start(f32[12,8,144]{2,1,0:T(8,128)S(1)} %get-tuple-element.37), channel_id=1, source_target_pairs={{0,1},{1,2},{2,3},{3,0},{4,5},{5,6},{6,7},{7,4},{8,9},{9,10},{10,1... | collective-permute-start | bytes 165896 | tf_op jit(solution)/shard_map/ppermute | solution.py:22
  52.0 4.7 %copy-start.2 = (f32[12,256,8]{2,1,0:T(8,128)S(1)}, f32[12,256,8]{2,1,0:T(8,128)}, u32[]{:S(2)}) copy-start(f32[12,256,8]{2,1,0:T(8,128)} %copy.42) | copy-start | bytes 294916
  57.9 1.7 %copy-start = (f32[12,272,144]{2,1,0:T(8,128)}, f32[12,272,144]{2,1,0:T(8,128)S(1)}, u32[]{:S(2)}) copy-start(f32[12,272,144]{2,1,0:T(8,128)S(1)} %pad_maximum_fusion) | copy-start | bytes 5640196
  60.3 1.2 slice-start
  61.5 1.9 %copy-start.1 = (f32[12,272,144]{2,1,0:T(8,128)S(1)}, f32[12,272,144]{2,1,0:T(8,128)}, u32[]{:S(2)}) copy-start(f32[12,272,144]{2,1,0:T(8,128)} %copy-done) | copy-start | bytes 5640196
  73.4 5.7 %copy-start.4 = (f32[2,256,128]{2,1,0:T(8,128)}, f32[2,256,128]{2,1,0:T(8,128)S(1)}, u32[]{:S(2)}) copy-start(f32[2,256,128]{2,1,0:T(8,128)S(1)} %get-tuple-element.17) | copy-start | bytes 786436
  74.3 48.9 %all-to-all-start.1 = ((f32[2,256,128]{2,0,1:T(2,128)}), f32[2,256,128]{2,0,1:T(2,128)S(1)}, u32[]{:S(2)}, u32[]{:S(2)}) async-start(f32[2,256,128]{2,0,1:T(2,128)} %copy.49), calls=%async_computation.1 | async-start | bytes 524288 | tf_op jit(solution)/shard_map/all_to_all | solution.py:164
where the time goes:
time: 125 us; the launch traced here: 124 us
  blocking collectives  40.1 us (32%)
  local copies, waits for them, and re-layouts  27.9 us (22%)
  waiting for transfers between devices  21.5 us (17%)
  other arithmetic  19.8 us (16%)
  starting transfers between devices  13.8 us (11%)
    psum x1, blocking collectives, record_sum(): global_sums.append(lax.psum(own_sum, ('gx', 'gy')))  40.1 us
    all_to_all x1, waiting for transfers between devices, local(): lax.all_to_all(ocean_forcing, 'gx', split_axis=2, concat_axis=1, tiled=True)  13 us
    unnamed x25, local copies, waits for them, and re-layouts  9.82 us
    all_to_all x1, starting transfers between devices, local(): lax.all_to_all(ocean_forcing, 'gx', split_axis=2, concat_axis=1, tiled=True)  7.41 us
    ppermute x2, waiting for transfers between devices, extended(): lax.ppermute(tail, axis, [(i, (i + 1) % count) for i in range(count)])  7.03 us
    all_to_all x3, local copies, waits for them, and re-layouts, local(): lax.all_to_all(ocean_forcing, 'gx', split_axis=2, concat_axis=1, tiled=True)  5.33 us
    another operation x8, other arithmetic, relax_stress(): jnp.stack([strength * (divergence / delta_rate - 1.0), strength * tension...  3.65 us
    all_to_all x1, starting transfers between devices, local(): lax.all_to_all(ice_stress, 'gx', split_axis=1, concat_axis=2, tiled=True)  3.41 us
  transfers between devices with their start and end apart: 6, of which 4 were waited for; matrix products, arithmetic and copies ran while one was open for 9% of the time, Pallas kernels for 0%

commit v1 on v0

v1 whole, which is shorter than its diff:
```python
import functools

import jax
import jax.numpy as jnp
from jax import lax
from jax.experimental import pallas as pl
from jax.experimental.pallas import tpu as pltpu
from jax.sharding import PartitionSpec as P

ITERS = 4
DELTA_FLOOR = 0.0025
PAD = 8
CH = 64
MESH = pl.DeviceIdType.MESH

WEST, EAST, SOUTH, NORTH, SW, SE, NW, NE = range(8)
STEPS = ((-1, 0), (1, 0), (0, -1), (0, 1), (-1, -1), (1, -1), (-1, 1), (1, 1))
OPPOSITE = (EAST, WEST, NORTH, SOUTH, NE, NW, SE, SW)


def rows_of(*rows):
    return jnp.concatenate(rows, axis=0)


def relaxed(east_dx, north_dx, east_dy, north_dy, stress, strength, ice):
    divergence = east_dx + north_dy
    tension = east_dx - north_dy
    shear = east_dy + north_dx
    inv = lax.rsqrt(divergence * divergence + 0.25 * (tension * tension + shear * shear) + DELTA_FLOOR)
    scaled = strength * inv
    return (
        (0.75 * stress[0] + 0.25 * (scaled * divergence - strength)) * ice,
        (0.75 * stress[1] + 0.0625 * (scaled * tension)) * ice,
        (0.75 * stress[2] + 0.03125 * (scaled * shear)) * ice,
    )


def drag_of(u, v, cu, cv):
    a = cu - u
    b = cv - v
    y = a * a + b * b + 0.01
    return y * lax.rsqrt(y)


def kernel(
    G, Y, R, C, B,
    vel_in, sig_in, mass_in, strength_in, mask_in, forcing_in,
    vel_out, sig_out, res_out, os_out,
    vel0, velb, sigb, mass, strength, ice, mask, forcing, ocean,
    pack, halo, turned,
    xs, xr, ys, yr, xs1, xr1, ys1, yr1, rs, rx, ry_s, ry,
    in_sem, f_send, f_recv, h_send, h_recv, i_send, i_recv, o_send, o_recv, r_send, r_recv, out_sem,
):
    gx = lax.axis_index("gx")
    gy = lax.axis_index("gy")

    def at(dx, dy):
        return {"gx": lax.rem(gx + dx + G, G), "gy": lax.rem(gy + dy + Y, Y)}

    inner = pl.ds(PAD, R)
    loads = [
        pltpu.make_async_copy(vel_in, velb.at[:, inner], in_sem.at[0]),
        pltpu.make_async_copy(sig_in, sigb.at[:, inner], in_sem.at[1]),
        pltpu.make_async_copy(strength_in, strength, in_sem.at[2]),
        pltpu.make_async_copy(mask_in, mask, in_sem.at[3]),
        pltpu.make_async_copy(vel_in, vel0, in_sem.at[4]),
        pltpu.make_async_copy(mass_in, mass, in_sem.at[5]),
    ]
    for copy in loads:
        copy.start()

    barrier = pltpu.get_barrier_semaphore()
    partners = [(d, 0) for d in range(1, G)] + [(0, d) for d in range(1, Y)] + list(STEPS[4:])
    for dx, dy in partners:
        pl.semaphore_signal(barrier, inc=1, device_id=at(dx, dy), device_id_type=MESH)
    pl.semaphore_wait(barrier, len(partners))

    mine = pl.ds(pl.multiple_of(gx * B, B), B)
    own_columns = pl.ds(pl.multiple_of(gx * C, C), C)
    own_forcing = pltpu.make_async_copy(forcing_in.at[:, :, own_columns], forcing.at[:, mine], f_recv.at[0])

    def send_forcing():
        sent = []
        for d in range(1, G):
            to = lax.rem(gx + d, G)
            copy = pltpu.make_async_remote_copy(
                src_ref=forcing_in.at[:, :, pl.ds(pl.multiple_of(to * C, C), C)],
                dst_ref=forcing.at[:, mine],
                send_sem=f_send.at[d],
                recv_sem=f_recv.at[d],
                device_id={"gx": to, "gy": gy},
                device_id_type=MESH,
            )
            copy.start()
            sent.append(copy)
        own_forcing.start()
        return sent

    def exchange(e):
        copies = []
        for n in range(8):
            src, dst = (xs.at[e], xr.at[e, n]) if n < 2 else (ys.at[e], yr.at[e, n - 2])
            slot = OPPOSITE[n]
            dst = xr.at[e, slot] if n < 2 else yr.at[e, slot - 2]
            copy = pltpu.make_async_remote_copy(
                src_ref=src, dst_ref=dst, send_sem=h_send.at[e, n], recv_sem=h_recv.at[e, slot],
                device_id=at(*STEPS[n]), device_id_type=MESH,
            )
            copy.start()
            copies.append(copy)
        return copies

    def arrive(e):
        for n in range(8):
            dst = xr.at[e, n] if n < 2 else yr.at[e, n - 2]
            pltpu.make_async_remote_copy(
                src_ref=dst, dst_ref=dst, send_sem=h_send.at[e, n], recv_sem=h_recv.at[e, n],
                device_id=at(*STEPS[n]), device_id_type=MESH,
            ).wait_recv()

    lanes = lax.broadcasted_iota(jnp.int32, (CH, C), 1)

    def pack_velocity(r0, u, v):
        pack[pl.ds(r0, CH), :] = jnp.where(
            lanes < 2, u,
            jnp.where(
                lanes < 4, pltpu.roll(v, 2, 1),
                jnp.where(lanes < 6, pltpu.roll(u, 6, 1), pltpu.roll(v, 8, 1)),
            ),
        )

    def chunks(body, init=0):
        def step(i, carry):
            return body(pl.multiple_of(i * CH, CH), carry)

        return lax.fori_loop(0, R // CH, step, init)

    def edge_rows(e):
        for q, (c, r) in enumerate(((0, 0), (0, 1), (1, 0), (1, 1), (0, R - 2), (0, R - 1), (1, R - 2), (1, R - 1))):
            ys[e, q : q + 1, :] = velb[c, PAD + r : PAD + r + 1, :]

    for copy in loads[:4]:
        copy.wait()

    def first_pack(r0, carry):
        rows = pl.ds(PAD + r0, CH)
        pack_velocity(r0, velb[0, rows, :], velb[1, rows, :])
        return carry

    chunks(first_pack)
    xs[0] = pack[...].T[0:8]
    edge_rows(0)
    started = exchange(0)

    def second_pack(r0, carry):
        rows = pl.ds(r0, CH)
        frac = mask[rows, :].astype(jnp.float32)
        ice[rows, :] = frac
        padded = pl.ds(PAD + r0, CH)
        fields = [sigb[0, padded, :], sigb[1, padded, :], sigb[2, padded, :], strength[rows, :], frac]
        out = jnp.zeros((CH, C), jnp.float32)
        for q, field in enumerate(fields):
            out = jnp.where(lanes == q, pltpu.roll(field, q, 1) if q else field, out)
            out = jnp.where(lanes == 8 + q, pltpu.roll(field, 9 + q, 1), out)
        pack[rows, :] = out
        return carry

    chunks(second_pack)
    xs1[...] = pack[...].T[0:16]
    ys1[...] = jnp.zeros_like(ys1)
    for q, r in ((0, 0), (8, R - 1)):
        for c in range(3):
            ys1[q + c : q + c + 1, :] = sigb[c, PAD + r : PAD + r + 1, :]
        ys1[q + 3 : q + 4, :] = strength[r : r + 1, :]
        ys1[q + 4 : q + 5, :] = ice[r : r + 1, :]
    fixed = []
    for n in range(4):
        slot = OPPOSITE[n]
        src, dst = (xs1, xr1.at[slot]) if n < 2 else (ys1, yr1.at[slot - 2])
        copy = pltpu.make_async_remote_copy(
            src_ref=src, dst_ref=dst, send_sem=i_send.at[n], recv_sem=i_recv.at[slot],
            device_id=at(*STEPS[n]), device_id_type=MESH,
        )
        copy.start()
        fixed.append(copy)
    sent_forcing = send_forcing()
    turned[...] = jnp.zeros_like(turned)

    has_south = (gy > 0).astype(jnp.float32)
    has_north = (gy < Y - 1).astype(jnp.float32)
    for copy in loads[4:]:
        copy.wait()
    for n in range(4):
        slot = OPPOSITE[n]
        dst = xr1.at[slot] if n < 2 else yr1.at[slot - 2]
        fixed[n].wait_recv()
    xw, xe, ysouth, ynorth = xr1[0], xr1[1], yr1[0], yr1[1]
    x_sig = [rows_of(xw[8 + c : 9 + c], xe[c : c + 1]) for c in range(3)]
    x_strength = rows_of(xw[11:12], xe[3:4])
    x_ice = rows_of(xw[12:13], xe[4:5])
    y_sig = [rows_of(ysouth[8 + c : 9 + c], ynorth[c : c + 1]) for c in range(3)]
    y_strength = rows_of(ysouth[11:12], ynorth[3:4])
    y_ice = rows_of(ysouth[12:13] * has_south, ynorth[4:5] * has_north)
    x_lane = lax.broadcasted_iota(jnp.int32, (4, R), 1)
    y_lane = lax.broadcasted_iota(jnp.int32, (4, C), 1)
    x_sign = jnp.where(lax.rem(lax.broadcasted_iota(jnp.int32, (4, R), 0), 2) == 0, 0.5, -0.5)
    y_sign = jnp.where(lax.rem(lax.broadcasted_iota(jnp.int32, (4, C), 0), 2) == 0, 0.5, -0.5)

    for k in range(ITERS):
        arrive(k)
        w, e = xr[k, 0], xr[k, 1]
        own = xs[k]
        s, n = yr[k, 0] * has_south, yr[k, 1] * has_north
        sw, se = yr[k, 2] * has_south, yr[k, 3] * has_south
        nw, ne = yr[k, 4] * has_north, yr[k, 5] * has_north
        own_y = ys[k]
        centre = rows_of(w[5:6], e[0:1], w[7:8], e[2:3])
        turned[0:4, :] = centre
        halo[...] = turned[...].T
        velb[0, PAD - 1 : PAD, :] = s[5:6]
        velb[1, PAD - 1 : PAD, :] = s[7:8]
        velb[0, PAD + R : PAD + R + 1, :] = n[0:1]
        velb[1, PAD + R : PAD + R + 1, :] = n[2:3]

        def sig_step(r0, carry):
            rows = pl.ds(r0, CH)
            mid = pl.ds(PAD + r0, CH)
            low = pl.ds(PAD - 1 + r0, CH)
            high = pl.ds(PAD + 1 + r0, CH)
            cols = halo[rows, :]
            slopes = []
            for c in range(2):
                f = velb[c, mid, :]
                right = jnp.where(lanes == C - 1, cols[:, 2 * c + 1 : 2 * c + 2], pltpu.roll(f, C - 1, 1))
                left = jnp.where(lanes == 0, cols[:, 2 * c : 2 * c + 1], pltpu.roll(f, 1, 1))
                slopes.append(0.5 * (right - left))
            for c in range(2):
                slopes.append(0.5 * (velb[c, high, :] - velb[c, low, :]))
            new = relaxed(
                slopes[0], slopes[1], slopes[2], slopes[3],
                [sigb[c, mid, :] for c in range(3)], strength[rows, :], ice[rows, :],
            )
            for c in range(3):
                sigb[c, mid, :] = new[c]
            return carry

        chunks(sig_step)

        x_dx = x_sign * (rows_of(own[0:1], own[5:6], own[2:3], own[7:8]) - rows_of(w[4:5], e[1:2], w[6:7], e[3:4]))

        def corner(a, b, q, lane_a, lane_b, length):
            parts = []
            for ref, row, lane in ((a, q[0], lane_a), (b, q[1], lane_b), (a, q[2], lane_a), (b, q[3], lane_b)):
                parts.append(jnp.broadcast_to(ref[row : row + 1, lane : lane + 1], (1, length)))
            return rows_of(*parts)

        below = jnp.where(x_lane == 0, corner(sw, se, (5, 5, 7, 7), C - 1, 0, R), pltpu.roll(centre, 1, 1))
        above = jnp.where(x_lane == R - 1, corner(nw, ne, (0, 0, 2, 2), C - 1, 0, R), pltpu.roll(centre, R - 1, 1))
        x_dy = 0.5 * (above - below)
        x_sig = relaxed(x_dx[0:2], x_dx[2:4], x_dy[0:2], x_dy[2:4], x_sig, x_strength, x_ice)

        centre_y = rows_of(s[5:6], n[0:1], s[7:8], n[2:3])
        y_dy = y_sign * (
            rows_of(own_y[0:1], own_y[5:6], own_y[2:3], own_y[7:8]) - rows_of(s[4:5], n[1:2], s[6:7], n[3:4])
        )
        left = jnp.where(y_lane == 0, corner(sw, nw, (5, 0, 7, 2), C - 1, C - 1, C), pltpu.roll(centre_y, 1, 1))
        right = jnp.where(y_lane == C - 1, corner(se, ne, (5, 0, 7, 2), 0, 0, C), pltpu.roll(centre_y, C - 1, 1))
        y_dx = 0.5 * (right - left)
        y_sig = relaxed(y_dx[0:2], y_dx[2:4], y_dy[0:2], y_dy[2:4], y_sig, y_strength, y_ice)
        for c in range(3):
            sigb[c, PAD - 1 : PAD, :] = y_sig[c][0:1]
            sigb[c, PAD + R : PAD + R + 1, :] = y_sig[c][1:2]
        turned[0:4, :] = rows_of(0.5 * (x_sig[0] + x_sig[1]), x_sig[2])
        halo[...] = turned[...].T
        if k == ITERS - 1:
            keep_sig = pltpu.make_async_copy(sigb.at[:, inner], sig_out, out_sem.at[0])
            keep_sig.start()

        if k == 0:
            own_forcing.wait()
            for copy in sent_forcing:
                copy.wait_recv()

        last = k == ITERS - 1

        def vel_step(r0, total):
            rows = pl.ds(r0, CH)
            mid = pl.ds(PAD + r0, CH)
            low = pl.ds(PAD - 1 + r0, CH)
            high = pl.ds(PAD + 1 + r0, CH)
            cols = halo[rows, :]
            sxx = 0.5 * (sigb[0, mid, :] + sigb[1, mid, :])
            sxy = sigb[2, mid, :]

            def dx(f, q):
                right = jnp.where(lanes == C - 1, cols[:, q + 1 : q + 2], pltpu.roll(f, C - 1, 1))
                left = jnp.where(lanes == 0, cols[:, q : q + 1], pltpu.roll(f, 1, 1))
                return 0.5 * (right - left)

            dy_xy = 0.5 * (sigb[2, high, :] - sigb[2, low, :])
            dy_yy = 0.25 * ((sigb[0, high, :] - sigb[1, high, :]) - (sigb[0, low, :] - sigb[1, low, :]))
            force_east = dx(sxx, 0) + dy_xy
            force_north = dx(sxy, 2) + dy_yy
            u = velb[0, mid, :]
            v = velb[1, mid, :]
            cu = forcing[2, rows, :]
            cv = forcing[3, rows, :]
            frac = ice[rows, :]
            drag = drag_of(u, v, cu, cv)
            if k == 0:
                inv_mass = 1.0 / mass[rows, :]
                mass[rows, :] = inv_mass
            else:
                inv_mass = mass[rows, :]
            inv_den = frac / (5.0 + drag * inv_mass)
            lat = (gy * R + r0 + lax.broadcasted_iota(jnp.int32, (CH, C), 0)).astype(jnp.float32)
            coriolis = 0.3 + 1.2 * (lat + 0.5) / (R * Y)
            new_u = (
                4.0 * u + vel0[0, rows, :] + (force_east + forcing[0, rows, :] + drag * cu) * inv_mass + coriolis * v
            ) * inv_den
            new_v = (
                4.0 * v + vel0[1, rows, :] + (force_north + forcing[1, rows, :] + drag * cv) * inv_mass - coriolis * u
            ) * inv_den
            velb[0, mid, :] = new_u
            velb[1, mid, :] = new_v
            if last:
                final = drag_of(new_u, new_v, cu, cv) * frac
                ocean[0, rows, :] = final * (new_u - cu)
                ocean[1, rows, :] = final * (new_v - cv)
            else:
                pack_velocity(r0, new_u, new_v)
            du = new_u - u
            dv = new_v - v
            return total + du * du + dv * dv

        total = chunks(vel_step, jnp.zeros((CH, C), jnp.float32))
        if not last:
            edge_rows(k + 1)
            xs[k + 1] = pack[...].T[0:8]
            started += exchange(k + 1)
        rs[k : k + 1, :] = jnp.sum(total, axis=0, keepdims=True)

    rs[ITERS:8, :] = jnp.zeros((8 - ITERS, C), jnp.float32)
    sums = []
    for d in range(1, G):
        copy = pltpu.make_async_remote_copy(
            src_ref=rs, dst_ref=rx.at[gx], send_sem=r_send.at[d], recv_sem=r_recv.at[d],
            device_id=at(d, 0), device_id_type=MESH,
        )
        copy.start()
        sums.append(copy)
    outs = []
    for d in range(1, G):
        to = lax.rem(gx + d, G)
        copy = pltpu.make_async_remote_copy(
            src_ref=ocean.at[:, pl.ds(pl.multiple_of(to * B, B), B)],
            dst_ref=os_out.at[:, :, own_columns],
            send_sem=o_send.at[d], recv_sem=o_recv.at[d],
            device_id={"gx": to, "gy": gy}, device_id_type=MESH,
        )
        copy.start()
        outs.append(copy)
    own_out = pltpu.make_async_copy(ocean.at[:, mine], os_out.at[:, :, own_columns], out_sem.at[1])
    own_out.start()
    keep_vel = pltpu.make_async_copy(velb.at[:, inner], vel_out, out_sem.at[2])
    keep_vel.start()
    for copy in sums:
        copy.wait_recv()
    rx[gx] = rs[...]
    total = rx[0]
    for d in range(1, G):
        total = total + rx[d]
    ry_s[...] = total
    ry[gy] = total
    for d in range(1, Y):
        copy = pltpu.make_async_remote_copy(
            src_ref=ry_s, dst_ref=ry.at[gy], send_sem=r_send.at[G + d], recv_sem=r_recv.at[G + d],
            device_id=at(0, d), device_id_type=MESH,
        )
        copy.start()
        sums.append(copy)
    for copy in sums[G - 1 :]:
        copy.wait_recv()
    total = ry[0]
    for d in range(1, Y):
        total = total + ry[d]
    for k in range(ITERS):
        res_out[k] = jnp.sum(total[k : k + 1])
    for copy in outs:
        copy.wait_recv()
    for copy in started + fixed + sent_forcing + outs + sums:
        copy.wait_send()
    own_out.wait()
    keep_vel.wait()
    keep_sig.wait()


def local(velocity, stress, ice_mass, strength, land_mask, ocean_forcing):
    G, Y = lax.axis_size("gx"), lax.axis_size("gy")
    R, C = velocity.shape[1:]
    B = ocean_forcing.shape[1]
    f32 = jnp.float32
    dma = pltpu.SemaphoreType.DMA
    any_space = pl.BlockSpec(memory_space=pl.ANY)
    return pl.pallas_call(
        functools.partial(kernel, G, Y, R, C, B),
        out_shape=(
            jax.ShapeDtypeStruct(velocity.shape, f32),
            jax.ShapeDtypeStruct(stress.shape, f32),
            jax.ShapeDtypeStruct((ITERS,), f32),
            jax.ShapeDtypeStruct((2,) + ocean_forcing.shape[1:], f32),
        ),
        in_specs=[any_space] * 6,
        out_specs=(any_space, any_space, pl.BlockSpec(memory_space=pltpu.SMEM), any_space),
        scratch_shapes=[
            pltpu.VMEM((2, R, C), f32),
            pltpu.VMEM((2, R + 2 * PAD, C), f32),
            pltpu.VMEM((3, R + 2 * PAD, C), f32),
            pltpu.VMEM((R, C), f32),
            pltpu.VMEM((R, C), f32),
            pltpu.VMEM((R, C), f32),
            pltpu.VMEM((R, C), jnp.int32),
            pltpu.VMEM((4, R, C), f32),
            pltpu.VMEM((2, R, C), f32),
            pltpu.VMEM((R, C), f32),
            pltpu.VMEM((R, C), f32),
            pltpu.VMEM((C, R), f32),
            pltpu.VMEM((ITERS, 8, R), f32),
            pltpu.VMEM((ITERS, 2, 8, R), f32),
            pltpu.VMEM((ITERS, 8, C), f32),
            pltpu.VMEM((ITERS, 6, 8, C), f32),
            pltpu.VMEM((16, R), f32),
            pltpu.VMEM((2, 16, R), f32),
            pltpu.VMEM((16, C), f32),
            pltpu.VMEM((2, 16, C), f32),
            pltpu.VMEM((8, C), f32),
            pltpu.VMEM((G, 8, C), f32),
            pltpu.VMEM((8, C), f32),
            pltpu.VMEM((Y, 8, C), f32),
            dma((6,)),
            dma((G,)),
            dma((G,)),
            dma((ITERS, 8)),
            dma((ITERS, 8)),
            dma((4,)),
            dma((4,)),
            dma((G,)),
            dma((G,)),
            dma((G + Y,)),
            dma((G + Y,)),
            dma((3,)),
        ],
        compiler_params=pltpu.CompilerParams(collective_id=0, has_side_effects=True),
    )(velocity, stress, ice_mass, strength, land_mask, ocean_forcing)


def solution(mesh):
    placed = (
        P(None, "gy", "gx"),
        P(None, "gy", "gx"),
        P("gy", "gx"),
        P("gy", "gx"),
        P("gy", "gx"),
        P(None, ("gy", "gx"), None),
    )
    return jax.shard_map(
        local,
        mesh=mesh,
        in_specs=placed,
        out_specs=(P(None, "gy", "gx"), P(None, "gy", "gx"), P(), P(None, ("gy", "gx"), None)),
        check_vma=False,
    )
```

time: 125 us -> 52.9 us (0.42)
  Pallas kernels: 0 us -> 48.4 us
  blocking collectives: 40.1 us -> 0 us
  local copies, waits for them, and re-layouts: 27.9 us -> 3.69 us
  waiting for transfers between devices: 21.5 us -> 0 us
  other arithmetic: 19.8 us -> 0 us
  starting transfers between devices: 13.8 us -> 0 us
    pallas_call x0 -> x1, Pallas kernels: none -> 48.4 us  [local(): pl.pallas_call(functools.partial(kernel, G, Y, R, C, B), out_shape=(jax.S...]
    psum x1 -> x0, blocking collectives: 40.1 us -> none  [record_sum(): global_sums.append(lax.psum(own_sum, ('gx', 'gy')))]
    all_to_all x2 -> x0, waiting for transfers between devices: 13 us -> none  [the longest x1 13 us: local(): lax.all_to_all(ocean_forcing, 'gx', split_axis=2, concat_axis=1, tiled=True)]
    all_to_all x2 -> x0, starting transfers between devices: 10.8 us -> none  [the longest x1 7.41 us: local(): lax.all_to_all(ocean_forcing, 'gx', split_axis=2, concat_axis=1, tiled=True)]
    ppermute x4 -> x0, waiting for transfers between devices: 8.47 us -> none  [the longest x2 7.03 us: extended(): lax.ppermute(tail, axis, [(i, (i + 1) % count) for i in range(count)])]
    slice x23 -> x0, local copies, waits for them, and re-layouts: 7.81 us -> none  [the longest x2 2.79 us: extended(): lax.slice_in_dim(cells, cells.shape[dim] - width, cells.shape[dim], axis=...]
    mul x17 -> x0, other arithmetic: 7.18 us -> none  [the longest x3 2.72 us: relax_velocity(): (BETA * vel[0] + vel_start[0] + (force_east + forcing[0] + drag_rate * fo...]
    another operation x9 -> x0, other arithmetic: 6.66 us -> none  [the longest x8 3.65 us: relax_stress(): jnp.stack([strength * (divergence / delta_rate - 1.0), strength * tension...]
  transfers between devices with their start and end apart: 6 -> 0, of which waited for: 4 -> 0; matrix products, arithmetic and copies ran while one was open for 9% -> 0% of each run, Pallas kernels for 0% -> 0%
where the time goes in v1:
time: 52.9 us; the launch traced here: 52.7 us
  Pallas kernels  48.4 us (91%)
  local copies, waits for them, and re-layouts  3.69 us (7%)
  between operations  0.65 us (1%)
    pallas_call x1, Pallas kernels, local(): pl.pallas_call(functools.partial(kernel, G, Y, R, C, B), out_shape=(jax.S...  48.4 us
    unnamed x10, local copies, waits for them, and re-layouts  3.69 us

profile of v1, /device:TPU:0, one launch (start us, length us, event | category | flops | bytes accessed | tf_op | source)
XLA Modules:
  0.0 52.7 jit_solution(7590512325320360069)
XLA Ops:
  0.6 48.4 %shard_map.93 = (f32[2,256,128]{2,1,0:T(8,128)}, f32[3,256,128]{2,1,0:T(8,128)}, f32[4]{0:T(128)}, f32[2,32,1024]{2,1,0:T(8,128)}) custom-call(f32[2,256,128]{2,1,0:T(8,128)} %vel_in.1, f32[3,256,128]{2,1,0:T(8,128)} %sig_in.1, f32[256,128]{1,0:T(8,128)} %mass_in.1, f32[256,128]{1,0:T(8,128)} %strength_in.1, s32[256,128]{1,0:T(8,128)} %mask_in.1, ...), custom_call_target="tpu_custom_call" | custom-call | tf_op jit(solution)/shard_map/pallas_call | solution.py:405
  49.0 0.0 copy-start
  49.0 1.7 %copy.14 = f32[2,256,128]{2,1,0:T(8,128)} copy(f32[2,256,128]{2,1,0:T(8,128)} %get-tuple-element.8) | data formatting | bytes 524288
  50.7 0.0 copy-done
  50.7 0.0 copy-start.2
  50.7 0.0 copy-start.1
  50.7 0.7 %copy.15 = f32[3,256,128]{2,1,0:T(8,128)} copy(f32[3,256,128]{2,1,0:T(8,128)S(1)} %copy-done) | data formatting | bytes 786432
  51.5 0.0 copy-done.2
  51.5 0.5 copy.16
  52.0 0.0 copy-done.1
  52.0 0.7 %copy.17 = f32[2,32,1024]{2,1,0:T(8,128)} copy(f32[2,32,1024]{2,1,0:T(8,128)S(1)} %copy-done.1) | data formatting | bytes 524288
Async XLA Ops:
  49.0 1.7 %copy-start = (f32[3,256,128]{2,1,0:T(8,128)S(1)}, f32[3,256,128]{2,1,0:T(8,128)}, u32[]{:S(2)}) copy-start(f32[3,256,128]{2,1,0:T(8,128)} %get-tuple-element.9) | copy-start | bytes 1179652
  50.7 0.8 %copy-start.2 = (f32[4]{0:T(128)S(1)}, f32[4]{0:T(128)}, u32[]{:S(2)}) copy-start(f32[4]{0:T(128)} %get-tuple-element.10) | copy-start | bytes 52
  50.7 1.3 %copy-start.1 = (f32[2,32,1024]{2,1,0:T(8,128)S(1)}, f32[2,32,1024]{2,1,0:T(8,128)}, u32[]{:S(2)}) copy-start(f32[2,32,1024]{2,1,0:T(8,128)} %get-tuple-element.11) | copy-start | bytes 786436

commit v2 on v1

v2 whole, which is shorter than its diff:
```python
import functools

import jax
import jax.numpy as jnp
from jax import lax
from jax.experimental import pallas as pl
from jax.experimental.pallas import tpu as pltpu
from jax.sharding import PartitionSpec as P

ITERS = 4
DELTA_FLOOR = 0.0025
DEEP = 8
PAD = 16
SIDE = 128
MESH = pl.DeviceIdType.MESH

WEST, EAST, SOUTH, NORTH, SW, SE, NW, NE = range(8)
STEPS = ((-1, 0), (1, 0), (0, -1), (0, 1), (-1, -1), (1, -1), (-1, 1), (1, 1))
OPPOSITE = (EAST, WEST, NORTH, SOUTH, NE, NW, SE, SW)


def rows_of(*rows):
    return jnp.concatenate(rows, axis=0)


def relaxed(east_dx, north_dx, east_dy, north_dy, stress, strength, ice):
    divergence = east_dx + north_dy
    tension = east_dx - north_dy
    shear = east_dy + north_dx
    inv = lax.rsqrt(divergence * divergence + 0.25 * (tension * tension + shear * shear) + DELTA_FLOOR)
    scaled = strength * inv
    return (
        (0.75 * stress[0] + 0.25 * (scaled * divergence - strength)) * ice,
        (0.75 * stress[1] + 0.0625 * (scaled * tension)) * ice,
        (0.75 * stress[2] + 0.03125 * (scaled * shear)) * ice,
    )


def drag_of(u, v, cu, cv):
    a = cu - u
    b = cv - v
    y = a * a + b * b + 0.01
    return y * lax.rsqrt(y)


def moved(u, v, start, force_east, force_north, fe, fn, cu, cv, inv_mass, coriolis, frac):
    drag = drag_of(u, v, cu, cv)
    inv_den = frac / (5.0 + drag * inv_mass)
    new_u = (4.0 * u + start[0] + (force_east + fe + drag * cu) * inv_mass + coriolis * v) * inv_den
    new_v = (4.0 * v + start[1] + (force_north + fn + drag * cv) * inv_mass - coriolis * u) * inv_den
    return new_u, new_v


def kernel(
    G, Y, R, C, B,
    vel_in, sig_in, mass_in, strength_in, mask_in, forcing_in,
    vel_out, sig_out, res_out, os_out,
    vel0, velb, sigb, mass, strength, ice, mask, bands, forcing, ocean,
    pack, halo, turned, low, high, strip, f_out, f_in, f_strip,
    rs, rx, ry_s, ry,
    in_sem, f_send, f_recv, s_send, s_recv, e_send, e_recv, h_send, h_recv, y_send, y_recv,
    o_send, o_recv, r_send, r_recv, out_sem,
):
    gx = lax.axis_index("gx")
    gy = lax.axis_index("gy")
    L = R + 2 * SIDE
    SHIFT = SIDE - PAD

    def at(dx, dy):
        return {"gx": lax.rem(gx + dx + G, G), "gy": lax.rem(gy + dy + Y, Y)}

    def remote(src, dst, send, recv, where):
        return pltpu.make_async_remote_copy(
            src_ref=src, dst_ref=dst, send_sem=send, recv_sem=recv, device_id=where, device_id_type=MESH
        )

    inner = pl.ds(PAD, R)
    loads = [
        pltpu.make_async_copy(vel_in, velb.at[:, inner], in_sem.at[0]),
        pltpu.make_async_copy(sig_in, sigb.at[:, inner], in_sem.at[1]),
        pltpu.make_async_copy(mass_in, mass.at[inner], in_sem.at[2]),
        pltpu.make_async_copy(strength_in, strength.at[inner], in_sem.at[3]),
        pltpu.make_async_copy(mask_in, mask.at[inner], in_sem.at[4]),
        pltpu.make_async_copy(forcing_in, bands, in_sem.at[5]),
    ]
    for copy in loads:
        copy.start()

    barrier = pltpu.get_barrier_semaphore()
    partners = [(dx, dy) for dy in range(Y) for dx in range(G) if (dx or dy) and (dx == 0 or dy in (0, 1, Y - 1))]
    for dx, dy in partners:
        pl.semaphore_signal(barrier, inc=1, device_id=at(dx, dy), device_id_type=MESH)

    for ref in (velb, sigb, forcing):
        for c in range(ref.shape[0]):
            for r in (0, PAD + R + DEEP):
                ref[c, r : r + DEEP, :] = jnp.zeros((DEEP, C), jnp.float32)
    for ref in (turned, pack, f_strip, f_out):
        ref[...] = jnp.zeros_like(ref)

    for copy in loads[:5]:
        copy.wait()
    fields = [velb.at[0], velb.at[1], sigb.at[0], sigb.at[1], sigb.at[2], mass, strength, mask]
    for q, field in enumerate(fields):
        t = field[PAD : PAD + R, :].astype(jnp.float32).T
        low[q] = t[0:DEEP]
        high[q] = t[C - DEEP : C]
    loads[5].wait()
    for c in range(G):
        t = bands[:, :, c * C : (c + 1) * C].reshape(4 * B, C).T
        f_out[(c + 1) % G, 0:DEEP, 0 : 4 * B] = t[C - DEEP : C]
        f_out[(c + G - 1) % G, DEEP : 2 * DEEP, 0 : 4 * B] = t[0:DEEP]
    f_in[gx] = f_out[gx]

    pl.semaphore_wait(barrier, len(partners))

    near, far = pl.ds(0, DEEP), pl.ds(DEEP, DEEP)
    centre, before, after = pl.ds(SIDE, R), pl.ds(0, SIDE), pl.ds(SIDE + R, SIDE)
    first, final_rows = pl.ds(0, SIDE), pl.ds(R - SIDE, SIDE)
    plan = (
        (WEST, low, strip.at[:, far, centre]),
        (EAST, high, strip.at[:, near, centre]),
        (SW, low.at[:, :, first], strip.at[:, far, after]),
        (SE, high.at[:, :, first], strip.at[:, near, after]),
        (NW, low.at[:, :, final_rows], strip.at[:, far, before]),
        (NE, high.at[:, :, final_rows], strip.at[:, near, before]),
    )
    started = []
    for n, (way, src, dst) in enumerate(plan):
        started.append(remote(src, dst, h_send.at[n], h_recv.at[n], at(*STEPS[way])))
    bottom, top = pl.ds(PAD, DEEP), pl.ds(PAD + R - DEEP, DEEP)
    under, over = pl.ds(PAD - DEEP, DEEP), pl.ds(PAD + R, DEEP)
    for n, ref in enumerate((velb, sigb, mass, strength, mask)):
        for m, (way, src, dst) in enumerate(((SOUTH, bottom, over), (NORTH, top, under))):
            a, b = (ref.at[:, src], ref.at[:, dst]) if len(ref.shape) == 3 else (ref.at[src], ref.at[dst])
            started.append(remote(a, b, y_send.at[2 * n + m], y_recv.at[2 * n + m], at(*STEPS[way])))

    mine = pl.ds(pl.multiple_of(gx * B, B), B)
    padded_mine = pl.ds(pl.multiple_of(PAD + gx * B, DEEP), B)
    own_columns = pl.ds(pl.multiple_of(gx * C, C), C)
    own_forcing = pltpu.make_async_copy(bands.at[:, :, own_columns], forcing.at[:, padded_mine], f_recv.at[0])
    for d in range(1, G):
        to = lax.rem(gx + d, G)
        columns = pl.ds(pl.multiple_of(to * C, C), C)
        started.append(remote(bands.at[:, :, columns], forcing.at[:, padded_mine], f_send.at[d], f_recv.at[d], at(d, 0)))
        started.append(remote(f_out.at[to], f_in.at[gx], s_send.at[d], s_recv.at[d], at(d, 0)))
    for copy in started:
        copy.start()
    own_forcing.start()

    def beyond(side):
        step, src, dst = ((1, pl.ds(B - DEEP, DEEP), under), (-1, near, over))[side]
        copies = []
        for d in range(G):
            where = {"gx": d, "gy": lax.rem(gy + step + Y, Y)}
            k = 2 * side
            copies.append(
                remote(bands.at[:, src, pl.ds(d * C, C)], forcing.at[:, dst], e_send.at[d, k], e_recv.at[k], where)
            )
            copies.append(remote(f_out.at[d], f_in.at[G + side], e_send.at[d, k + 1], e_recv.at[k + 1], where))
        return copies

    edges = ((G - 1, 0), (0, 1))
    for holder, side in edges:

        @pl.when(gx == holder)
        def _():
            for copy in beyond(side):
                copy.start()

    for copy in started[:16]:
        copy.wait_recv()
    for copy in started[6:16]:
        copy.wait_send()

    has_south = (gy > 0).astype(jnp.float32)
    has_north = (gy < Y - 1).astype(jnp.float32)
    for c in range(2):
        velb[c, under, :] = velb[c, under, :] * has_south
        velb[c, over, :] = velb[c, over, :] * has_north
    ice[...] = mask[...].astype(jnp.float32)
    ice[under, :] = ice[under, :] * has_south
    ice[over, :] = ice[over, :] * has_north
    for c in range(2):
        vel0[c] = velb[c, PAD - DEEP : PAD + R + DEEP, :]

    strip_lane = lax.broadcasted_iota(jnp.int32, (2 * DEEP, L), 1)
    strip_row = lax.broadcasted_iota(jnp.int32, (2 * DEEP, L), 0)
    lat_s = strip_lane - SIDE + gy * R
    inside = ((lat_s >= 0) & (lat_s < R * Y)).astype(jnp.float32)
    cor_s = 0.3 + 1.2 * (lat_s.astype(jnp.float32) + 0.5) / (R * Y)
    sv = [strip[0] * inside, strip[1] * inside]
    sv0 = list(sv)
    ss = [strip[2], strip[3], strip[4]]
    s_strength = strip[6]
    s_ice = strip[7] * inside
    s_inv_mass = 1.0 / strip[5]

    def strip_dx(f, lo, hi):
        right = jnp.where(strip_row == DEEP - 1, lo, pltpu.roll(f, 2 * DEEP - 1, 0))
        left = jnp.where(strip_row == DEEP, hi, pltpu.roll(f, 1, 0))
        return 0.5 * (right - left)

    def strip_dy(f):
        return 0.5 * (pltpu.roll(f, L - 1, 1) - pltpu.roll(f, 1, 1))

    pieces = ((PAD - DEEP, DEEP), (PAD + R, DEEP)) + tuple((PAD + r, R // 2) for r in range(0, R, R // 2))

    def lane_of(n):
        return lax.broadcasted_iota(jnp.int32, (n, C), 1)

    def pack_pair(p, n, a, b):
        lane = lane_of(n)
        pack[p + SHIFT : p + SHIFT + n, :] = jnp.where(
            lane < 1, a, jnp.where(lane < 2, pltpu.roll(a, 2, 1), jnp.where(lane < 3, pltpu.roll(b, 2, 1), pltpu.roll(b, 4, 1)))
        )

    def ring(a, b):
        turned[0:2, :] = a[DEEP - 1 : DEEP + 1]
        turned[2:4, :] = b[DEEP - 1 : DEEP + 1]
        halo[...] = turned[...].T

    def main_dx(f, cols, q, lane):
        right = jnp.where(lane == C - 1, cols[:, q + 1 : q + 2], pltpu.roll(f, C - 1, 1))
        left = jnp.where(lane == 0, cols[:, q : q + 1], pltpu.roll(f, 1, 1))
        return 0.5 * (right - left)

    for p, n in pieces:
        pack_pair(p, n, velb[0, p : p + n, :], velb[1, p : p + n, :])

    for k in range(ITERS):
        last = k == ITERS - 1
        edge = pack[...].T[0:8]
        ring(sv[0], sv[1])
        for p, n in pieces:
            lane = lane_of(n)
            cols = halo[p + SHIFT : p + SHIFT + n, :]
            slopes = [main_dx(velb[c, p : p + n, :], cols, 2 * c, lane) for c in range(2)]
            slopes += [0.5 * (velb[c, p + 1 : p + n + 1, :] - velb[c, p - 1 : p + n - 1, :]) for c in range(2)]
            new = relaxed(
                *slopes, [sigb[c, p : p + n, :] for c in range(3)], strength[p : p + n, :], ice[p : p + n, :]
            )
            for c in range(3):
                sigb[c, p : p + n, :] = new[c]
            pack_pair(p, n, 0.5 * (new[0] + new[1]), new[2])
        if last:
            keep_sig = pltpu.make_async_copy(sigb.at[:, inner], sig_out, out_sem.at[0])
            keep_sig.start()
        ss = relaxed(
            strip_dx(sv[0], edge[0:1], edge[1:2]), strip_dx(sv[1], edge[2:3], edge[3:4]),
            strip_dy(sv[0]), strip_dy(sv[1]), ss, s_strength, s_ice,
        )
        s_xx = 0.5 * (ss[0] + ss[1])
        edge = pack[...].T[0:8]
        ring(s_xx, ss[2])

        if k == 0:
            own_forcing.wait()
            for copy in started[16:]:
                copy.wait_recv()
            for side in range(2):
                for copy, slot in ((0, forcing.at[:, (under, over)[side]]), (1, f_in.at[G + side])):
                    m = 2 * side + copy
                    remote(slot, slot, e_send.at[0, m], e_recv.at[m], at(0, 1)).wait_recv()
            for f in range(4):
                for b in range(-1, G + 1):
                    slot = G if b < 0 else G + 1 if b == G else b
                    a = SIDE + b * B
                    f_strip[f, :, a : a + B] = f_in[slot, :, f * B : (f + 1) * B]

        total = jnp.zeros((R // 2, C), jnp.float32)
        for p, n in pieces:
            if last and n == DEEP:
                continue
            lane = lane_of(n)
            cols = halo[p + SHIFT : p + SHIFT + n, :]
            sxx = 0.5 * (sigb[0, p : p + n, :] + sigb[1, p : p + n, :])
            sxy = sigb[2, p : p + n, :]
            hi, lo = pl.ds(p + 1, n), pl.ds(p - 1, n)
            dy_xy = 0.5 * (sigb[2, hi, :] - sigb[2, lo, :])
            dy_yy = 0.25 * ((sigb[0, hi, :] - sigb[1, hi, :]) - (sigb[0, lo, :] - sigb[1, lo, :]))
            force_east = main_dx(sxx, cols, 0, lane) + dy_xy
            force_north = main_dx(sxy, cols, 2, lane) + dy_yy
            u, v = velb[0, p : p + n, :], velb[1, p : p + n, :]
            fe, fn, cu, cv = (forcing[c, p : p + n, :] for c in range(4))
            frac = ice[p : p + n, :]
            if k == 0:
                inv_mass = 1.0 / mass[p : p + n, :]
                mass[p : p + n, :] = inv_mass
            else:
                inv_mass = mass[p : p + n, :]
            lat = (gy * R + (p - PAD) + lax.broadcasted_iota(jnp.int32, (n, C), 0)).astype(jnp.float32)
            coriolis = 0.3 + 1.2 * (lat + 0.5) / (R * Y)
            start = [vel0[c, p - PAD + DEEP : p - PAD + DEEP + n, :] for c in range(2)]
            new_u, new_v = moved(u, v, start, force_east, force_north, fe, fn, cu, cv, inv_mass, coriolis, frac)
            velb[0, p : p + n, :] = new_u
            velb[1, p : p + n, :] = new_v
            if last:
                drag = drag_of(new_u, new_v, cu, cv) * frac
                ocean[0, p - PAD : p - PAD + n, :] = drag * (new_u - cu)
                ocean[1, p - PAD : p - PAD + n, :] = drag * (new_v - cv)
            else:
                pack_pair(p, n, new_u, new_v)
            if n > DEEP:
                du = new_u - u
                dv = new_v - v
                total = total + (du * du + dv * dv)
        rs[k : k + 1, :] = jnp.sum(total, axis=0, keepdims=True)
        if not last:
            s_yy = 0.5 * (ss[0] - ss[1])
            force_east = strip_dx(s_xx, edge[0:1], edge[1:2]) + strip_dy(ss[2])
            force_north = strip_dx(ss[2], edge[2:3], edge[3:4]) + strip_dy(s_yy)
            sv = list(
                moved(
                    sv[0], sv[1], sv0, force_east, force_north,
                    f_strip[0], f_strip[1], f_strip[2], f_strip[3], s_inv_mass, cor_s, s_ice,
                )
            )

    rs[ITERS:8, :] = jnp.zeros((8 - ITERS, C), jnp.float32)
    sums = []
    for d in range(1, G):
        copy = pltpu.make_async_remote_copy(
            src_ref=rs, dst_ref=rx.at[gx], send_sem=r_send.at[d], recv_sem=r_recv.at[d],
            device_id=at(d, 0), device_id_type=MESH,
        )
        copy.start()
        sums.append(copy)
    outs = []
    for d in range(1, G):
        to = lax.rem(gx + d, G)
        copy = pltpu.make_async_remote_copy(
            src_ref=ocean.at[:, pl.ds(pl.multiple_of(to * B, B), B)],
            dst_ref=os_out.at[:, :, own_columns],
            send_sem=o_send.at[d], recv_sem=o_recv.at[d],
            device_id={"gx": to, "gy": gy}, device_id_type=MESH,
        )
        copy.start()
        outs.append(copy)
    own_out = pltpu.make_async_copy(ocean.at[:, mine], os_out.at[:, :, own_columns], out_sem.at[1])
    own_out.start()
    keep_vel = pltpu.make_async_copy(velb.at[:, inner], vel_out, out_sem.at[2])
    keep_vel.start()
    for copy in sums:
        copy.wait_recv()
    rx[gx] = rs[...]
    total = rx[0]
    for d in range(1, G):
        total = total + rx[d]
    ry_s[...] = total
    ry[gy] = total
    for d in range(1, Y):
        copy = pltpu.make_async_remote_copy(
            src_ref=ry_s, dst_ref=ry.at[gy], send_sem=r_send.at[G + d], recv_sem=r_recv.at[G + d],
            device_id=at(0, d), device_id_type=MESH,
        )
        copy.start()
        sums.append(copy)
    for copy in sums[G - 1 :]:
        copy.wait_recv()
    total = ry[0]
    for d in range(1, Y):
        total = total + ry[d]
    for k in range(ITERS):
        res_out[k] = jnp.sum(total[k : k + 1])
    for copy in outs:
        copy.wait_recv()
    for copy in started[:6] + started[16:] + outs + sums:
        copy.wait_send()
    for holder, side in edges:

        @pl.when(gx == holder)
        def _():
            for copy in beyond(side):
                copy.wait_send()

    own_out.wait()
    keep_vel.wait()
    keep_sig.wait()


def local(velocity, stress, ice_mass, strength, land_mask, ocean_forcing):
    G, Y = lax.axis_size("gx"), lax.axis_size("gy")
    R, C = velocity.shape[1:]
    B = ocean_forcing.shape[1]
    L = R + 2 * SIDE
    f32 = jnp.float32
    dma = pltpu.SemaphoreType.DMA
    any_space = pl.BlockSpec(memory_space=pl.ANY)
    return pl.pallas_call(
        functools.partial(kernel, G, Y, R, C, B),
        out_shape=(
            jax.ShapeDtypeStruct(velocity.shape, f32),
            jax.ShapeDtypeStruct(stress.shape, f32),
            jax.ShapeDtypeStruct((ITERS,), f32),
            jax.ShapeDtypeStruct((2,) + ocean_forcing.shape[1:], f32),
        ),
        in_specs=[any_space] * 6,
        out_specs=(any_space, any_space, pl.BlockSpec(memory_space=pltpu.SMEM), any_space),
        scratch_shapes=[
            pltpu.VMEM((2, R + 2 * DEEP, C), f32),
            pltpu.VMEM((2, R + 2 * PAD, C), f32),
            pltpu.VMEM((3, R + 2 * PAD, C), f32),
            pltpu.VMEM((R + 2 * PAD, C), f32),
            pltpu.VMEM((R + 2 * PAD, C), f32),
            pltpu.VMEM((R + 2 * PAD, C), f32),
            pltpu.VMEM((R + 2 * PAD, C), jnp.int32),
            pltpu.VMEM(ocean_forcing.shape, f32),
            pltpu.VMEM((4, R + 2 * PAD, C), f32),
            pltpu.VMEM((2, R, C), f32),
            pltpu.VMEM((L, C), f32),
            pltpu.VMEM((L, C), f32),
            pltpu.VMEM((C, L), f32),
            pltpu.VMEM((8, DEEP, R), f32),
            pltpu.VMEM((8, DEEP, R), f32),
            pltpu.VMEM((8, 2 * DEEP, L), f32),
            pltpu.VMEM((G, 2 * DEEP, SIDE), f32),
            pltpu.VMEM((G + 2, 2 * DEEP, SIDE), f32),
            pltpu.VMEM((4, 2 * DEEP, L), f32),
            pltpu.VMEM((8, C), f32),
            pltpu.VMEM((G, 8, C), f32),
            pltpu.VMEM((8, C), f32),
            pltpu.VMEM((Y, 8, C), f32),
            dma((6,)),
            dma((G,)),
            dma((G,)),
            dma((G,)),
            dma((G,)),
            dma((G, 4)),
            dma((4,)),
            dma((6,)),
            dma((6,)),
            dma((10,)),
            dma((10,)),
            dma((G,)),
            dma((G,)),
            dma((G + Y,)),
            dma((G + Y,)),
            dma((3,)),
        ],
        compiler_params=pltpu.CompilerParams(collective_id=0, has_side_effects=True),
    )(velocity, stress, ice_mass, strength, land_mask, ocean_forcing)


def solution(mesh):
    placed = (
        P(None, "gy", "gx"),
        P(None, "gy", "gx"),
        P("gy", "gx"),
        P("gy", "gx"),
        P("gy", "gx"),
        P(None, ("gy", "gx"), None),
    )
    return jax.shard_map(
        local,
        mesh=mesh,
        in_specs=placed,
        out_specs=(P(None, "gy", "gx"), P(None, "gy", "gx"), P(), P(None, ("gy", "gx"), None)),
        check_vma=False,
    )
```

time: 52.9 us -> 46.3 us (0.88)
  Pallas kernels: 48.4 us -> 41.8 us
    pallas_call x1, Pallas kernels: 48.4 us -> 41.8 us  [local(): pl.pallas_call(functools.partial(kernel, G, Y, R, C, B), out_shape=(jax.S...]
where the time goes in v2:
time: 46.3 us; the launch traced here: 46.2 us
  Pallas kernels  41.8 us (90%)
  local copies, waits for them, and re-layouts  3.69 us (8%)
  between operations  0.65 us (1%)
    pallas_call x1, Pallas kernels, local(): pl.pallas_call(functools.partial(kernel, G, Y, R, C, B), out_shape=(jax.S...  41.8 us
    unnamed x10, local copies, waits for them, and re-layouts  3.69 us

profile of v2, /device:TPU:0, one launch (start us, length us, event | category | flops | bytes accessed | tf_op | source)
XLA Modules:
  0.0 46.2 jit_solution(17198798273768612081)
XLA Ops:
  0.6 41.8 %shard_map.93 = (f32[2,256,128]{2,1,0:T(8,128)}, f32[3,256,128]{2,1,0:T(8,128)}, f32[4]{0:T(128)}, f32[2,32,1024]{2,1,0:T(8,128)}) custom-call(f32[2,256,128]{2,1,0:T(8,128)} %vel_in.1, f32[3,256,128]{2,1,0:T(8,128)} %sig_in.1, f32[256,128]{1,0:T(8,128)} %mass_in.1, f32[256,128]{1,0:T(8,128)} %strength_in.1, s32[256,128]{1,0:T(8,128)} %mask_in.1, ...), custom_call_target="tpu_custom_call" | custom-call | tf_op jit(solution)/shard_map/pallas_call | solution.py:390
  42.5 0.0 copy-start
  42.5 1.7 %copy.14 = f32[2,256,128]{2,1,0:T(8,128)} copy(f32[2,256,128]{2,1,0:T(8,128)} %get-tuple-element.8) | data formatting | bytes 524288
  44.2 0.0 copy-done
  44.2 0.0 copy-start.2
  44.2 0.0 copy-start.1
  44.2 0.7 %copy.15 = f32[3,256,128]{2,1,0:T(8,128)} copy(f32[3,256,128]{2,1,0:T(8,128)S(1)} %copy-done) | data formatting | bytes 786432
  44.9 0.0 copy-done.2
  45.0 0.5 %copy.16 = f32[4]{0:T(128)} copy(f32[4]{0:T(128)S(1)} %copy-done.2) | data formatting | bytes 32
  45.5 0.0 copy-done.1
  45.5 0.7 %copy.17 = f32[2,32,1024]{2,1,0:T(8,128)} copy(f32[2,32,1024]{2,1,0:T(8,128)S(1)} %copy-done.1) | data formatting | bytes 524288
Async XLA Ops:
  42.5 1.7 %copy-start = (f32[3,256,128]{2,1,0:T(8,128)S(1)}, f32[3,256,128]{2,1,0:T(8,128)}, u32[]{:S(2)}) copy-start(f32[3,256,128]{2,1,0:T(8,128)} %get-tuple-element.9) | copy-start | bytes 1179652
  44.2 0.8 %copy-start.2 = (f32[4]{0:T(128)S(1)}, f32[4]{0:T(128)}, u32[]{:S(2)}) copy-start(f32[4]{0:T(128)} %get-tuple-element.10) | copy-start | bytes 52
  44.2 1.3 %copy-start.1 = (f32[2,32,1024]{2,1,0:T(8,128)S(1)}, f32[2,32,1024]{2,1,0:T(8,128)}, u32[]{:S(2)}) copy-start(f32[2,32,1024]{2,1,0:T(8,128)} %get-tuple-element.11) | copy-start | bytes 786436

commit v3 on v2

--- a/solution.py
+++ b/solution.py
@@ -57,7 +57,7 @@
     vel_out, sig_out, res_out, os_out,
     vel0, velb, sigb, mass, strength, ice, mask, bands, forcing, ocean,
     pack, halo, turned, low, high, strip, f_out, f_in, f_strip,
-    rs, rx, ry_s, ry,
+    rs, rx,
     in_sem, f_send, f_recv, s_send, s_recv, e_send, e_recv, h_send, h_recv, y_send, y_recv,
     o_send, o_recv, r_send, r_recv, out_sem,
 ):
@@ -87,7 +87,7 @@
         copy.start()
 
     barrier = pltpu.get_barrier_semaphore()
-    partners = [(dx, dy) for dy in range(Y) for dx in range(G) if (dx or dy) and (dx == 0 or dy in (0, 1, Y - 1))]
+    partners = [(dx, dy) for dy in range(Y) for dx in range(G) if dx or dy]
     for dx, dy in partners:
         pl.semaphore_signal(barrier, inc=1, device_id=at(dx, dy), device_id_type=MESH)
 
@@ -139,7 +139,7 @@
     padded_mine = pl.ds(pl.multiple_of(PAD + gx * B, DEEP), B)
     own_columns = pl.ds(pl.multiple_of(gx * C, C), C)
     own_forcing = pltpu.make_async_copy(bands.at[:, :, own_columns], forcing.at[:, padded_mine], f_recv.at[0])
-    for d in range(1, G):
+    for d in sorted(range(1, G), key=lambda d: -abs(2 * d - G)):
         to = lax.rem(gx + d, G)
         columns = pl.ds(pl.multiple_of(to * C, C), C)
         started.append(remote(bands.at[:, :, columns], forcing.at[:, padded_mine], f_send.at[d], f_recv.at[d], at(d, 0)))
@@ -228,6 +228,8 @@
     for p, n in pieces:
         pack_pair(p, n, velb[0, p : p + n, :], velb[1, p : p + n, :])
 
+    sum_lane = lax.broadcasted_iota(jnp.int32, (1, C), 1)
+    own_sums = jnp.zeros((1, C), jnp.float32)
     for k in range(ITERS):
         last = k == ITERS - 1
         edge = pack[...].T[0:8]
@@ -305,7 +307,7 @@
                 du = new_u - u
                 dv = new_v - v
                 total = total + (du * du + dv * dv)
-        rs[k : k + 1, :] = jnp.sum(total, axis=0, keepdims=True)
+        own_sums = jnp.where(sum_lane == k, jnp.sum(total), own_sums)
         if not last:
             s_yy = 0.5 * (ss[0] - ss[1])
             force_east = strip_dx(s_xx, edge[0:1], edge[1:2]) + strip_dy(ss[2])
@@ -317,17 +319,16 @@
                 )
             )
 
-    rs[ITERS:8, :] = jnp.zeros((8 - ITERS, C), jnp.float32)
+    rs[...] = own_sums
+    here = gx * Y + gy
     sums = []
-    for d in range(1, G):
-        copy = pltpu.make_async_remote_copy(
-            src_ref=rs, dst_ref=rx.at[gx], send_sem=r_send.at[d], recv_sem=r_recv.at[d],
-            device_id=at(d, 0), device_id_type=MESH,
-        )
+    for n, (dx, dy) in enumerate(partners):
+        copy = remote(rs, rx.at[here], r_send.at[n], r_recv.at[n], at(dx, dy))
         copy.start()
         sums.append(copy)
+    rx[here] = own_sums
     outs = []
-    for d in range(1, G):
+    for d in sorted(range(1, G), key=lambda d: -abs(2 * d - G)):
         to = lax.rem(gx + d, G)
         copy = pltpu.make_async_remote_copy(
             src_ref=ocean.at[:, pl.ds(pl.multiple_of(to * B, B), B)],
@@ -343,26 +344,9 @@
     keep_vel.start()
     for copy in sums:
         copy.wait_recv()
-    rx[gx] = rs[...]
-    total = rx[0]
-    for d in range(1, G):
-        total = total + rx[d]
-    ry_s[...] = total
-    ry[gy] = total
-    for d in range(1, Y):
-        copy = pltpu.make_async_remote_copy(
-            src_ref=ry_s, dst_ref=ry.at[gy], send_sem=r_send.at[G + d], recv_sem=r_recv.at[G + d],
-            device_id=at(0, d), device_id_type=MESH,
-        )
-        copy.start()
-        sums.append(copy)
-    for copy in sums[G - 1 :]:
-        copy.wait_recv()
-    total = ry[0]
-    for d in range(1, Y):
-        total = total + ry[d]
+    total = jnp.sum(rx[...], axis=0)
     for k in range(ITERS):
-        res_out[k] = jnp.sum(total[k : k + 1])
+        res_out[k] = jnp.sum(jnp.where(sum_lane == k, total, 0.0))
     for copy in outs:
         copy.wait_recv()
     for copy in started[:6] + started[16:] + outs + sums:
@@ -417,10 +401,8 @@
             pltpu.VMEM((G, 2 * DEEP, SIDE), f32),
             pltpu.VMEM((G + 2, 2 * DEEP, SIDE), f32),
             pltpu.VMEM((4, 2 * DEEP, L), f32),
-            pltpu.VMEM((8, C), f32),
-            pltpu.VMEM((G, 8, C), f32),
-            pltpu.VMEM((8, C), f32),
-            pltpu.VMEM((Y, 8, C), f32),
+            pltpu.VMEM((1, C), f32),
+            pltpu.VMEM((G * Y, 1, C), f32),
             dma((6,)),
             dma((G,)),
             dma((G,)),
@@ -434,8 +416,8 @@
             dma((10,)),
             dma((G,)),
             dma((G,)),
-            dma((G + Y,)),
-            dma((G + Y,)),
+            dma((G * Y,)),
+            dma((G * Y,)),
             dma((3,)),
         ],
         compiler_params=pltpu.CompilerParams(collective_id=0, has_side_effects=True),

time: 46.3 us -> 45.5 us (0.983)
  Pallas kernels: 41.8 us -> 41 us
    pallas_call x1, Pallas kernels: 41.8 us -> 41 us  [local(): pl.pallas_call(functools.partial(kernel, G, Y, R, C, B), out_shape=(jax.S...]
where the time goes in v3:
time: 45.5 us; the launch traced here: 45.3 us
  Pallas kernels  41 us (90%)
  local copies, waits for them, and re-layouts  3.69 us (8%)
  between operations  0.65 us (1%)
    pallas_call x1, Pallas kernels, local(): pl.pallas_call(functools.partial(kernel, G, Y, R, C, B), out_shape=(jax.S...  41 us
    unnamed x10, local copies, waits for them, and re-layouts  3.69 us

profile of v3, /device:TPU:0, one launch (start us, length us, event | category | flops | bytes accessed | tf_op | source)
XLA Modules:
  0.0 45.3 jit_solution(7463373204677065761)
XLA Ops:
  0.6 41.0 %shard_map.93 = (f32[2,256,128]{2,1,0:T(8,128)}, f32[3,256,128]{2,1,0:T(8,128)}, f32[4]{0:T(128)}, f32[2,32,1024]{2,1,0:T(8,128)}) custom-call(f32[2,256,128]{2,1,0:T(8,128)} %vel_in.1, f32[3,256,128]{2,1,0:T(8,128)} %sig_in.1, f32[256,128]{1,0:T(8,128)} %mass_in.1, f32[256,128]{1,0:T(8,128)} %strength_in.1, s32[256,128]{1,0:T(8,128)} %mask_in.1, ...), custom_call_target="tpu_custom_call" | custom-call | tf_op jit(solution)/shard_map/pallas_call | solution.py:374
  41.6 0.0 copy-start
  41.6 1.7 %copy.14 = f32[2,256,128]{2,1,0:T(8,128)} copy(f32[2,256,128]{2,1,0:T(8,128)} %get-tuple-element.8) | data formatting | bytes 524288
  43.3 0.0 copy-done
  43.3 0.0 copy-start.2
  43.3 0.0 copy-start.1
  43.3 0.7 %copy.15 = f32[3,256,128]{2,1,0:T(8,128)} copy(f32[3,256,128]{2,1,0:T(8,128)S(1)} %copy-done) | data formatting | bytes 786432
  44.1 0.0 copy-done.2
  44.1 0.5 %copy.16 = f32[4]{0:T(128)} copy(f32[4]{0:T(128)S(1)} %copy-done.2) | data formatting | bytes 32
  44.6 0.0 copy-done.1
  44.6 0.7 %copy.17 = f32[2,32,1024]{2,1,0:T(8,128)} copy(f32[2,32,1024]{2,1,0:T(8,128)S(1)} %copy-done.1) | data formatting | bytes 524288
Async XLA Ops:
  41.6 1.7 %copy-start = (f32[3,256,128]{2,1,0:T(8,128)S(1)}, f32[3,256,128]{2,1,0:T(8,128)}, u32[]{:S(2)}) copy-start(f32[3,256,128]{2,1,0:T(8,128)} %get-tuple-element.9) | copy-start | bytes 1179652
  43.3 0.8 %copy-start.2 = (f32[4]{0:T(128)S(1)}, f32[4]{0:T(128)}, u32[]{:S(2)}) copy-start(f32[4]{0:T(128)} %get-tuple-element.10) | copy-start | bytes 52
  43.3 1.3 %copy-start.1 = (f32[2,32,1024]{2,1,0:T(8,128)S(1)}, f32[2,32,1024]{2,1,0:T(8,128)}, u32[]{:S(2)}) copy-start(f32[2,32,1024]{2,1,0:T(8,128)} %get-tuple-element.11) | copy-start | bytes 786436
